TPU v7x, 32 devices: a whole 2x2x4 slice. The times are simulated.
32 devices in a mesh: dp: 8 (over z, core), seq: 4 (over y, x).
Axes of the slice: x: 2, y: 2, z: 4, core: 2. Of those that a mesh axis runs over, the one named last changes fastest.
Arguments:
- tokens: bfloat16 [32, 256, 1024], P(('dp', 'seq')), may hold values from -6 to 6
- queries: bfloat16 [32, 256, 1024], P(('dp', 'seq')), may hold values from -240 to 240
- keys: bfloat16 [32, 256, 1024], P(('dp', 'seq')), may hold values from -7 to 7
- values: bfloat16 [32, 256, 1024], P(('dp', 'seq')), may hold values from -6 to 6
- ln_gain: bfloat16 [1024], replicated, may hold values from 0.5 to 1.5
- mean_in: bfloat16 [1024, 2048], P(None, 'seq'), may hold values from -0.1875 to 0.1875
- sigma_in: bfloat16 [1024, 2048], P(None, 'seq'), may hold values from 0.0039978027 to 0.029907227
- noise_in: bfloat16 [1024, 2048], P(None, 'seq'), may hold values from -4 to 4
- mean_out: bfloat16 [2048, 1024], P('seq'), may hold values from -0.125 to 0.125
- sigma_out: bfloat16 [2048, 1024], P('seq'), may hold values from 0.0019989014 to 0.014953613
- noise_out: bfloat16 [2048, 1024], P('seq'), may hold values from -4 to 4
- flip_in: int32 [32, 1024], P('dp'), may hold values from -1 to 1, as said below
- flip_mid: int32 [32, 2048], P('dp', 'seq'), may hold values from -1 to 1, as said below
- flip_hidden: int32 [32, 2048], P('dp', 'seq'), may hold values from -1 to 1, as said below
- flip_out: int32 [32, 1024], P('dp'), may hold values from -1 to 1, as said below
- cotangent: bfloat16 [32, 256, 1024], P(('dp', 'seq')), may hold values from -0.75 to 0.75
Outputs:
- block_out: bfloat16 [32, 256, 1024], P(('dp', 'seq'))
- resid_grad: bfloat16 [32, 256, 1024], P(('dp', 'seq'))
- grad_mean_in: float32 [1024, 2048], P(None, 'seq')
- grad_sigma_in: float32 [1024, 2048], P(None, 'seq')
- grad_mean_out: float32 [2048, 1024], P('seq')
- grad_sigma_out: float32 [2048, 1024], P('seq')
Inputs may be any that keep to these rules, and one draw needn't show every extreme that they name: `flip_in`: each entry is -1 or +1. `flip_mid`: each entry is -1 or +1. `flip_hidden`: each entry is -1 or +1. `flip_out`: each entry is -1 or +1.
All inputs are finite; a program needn't handle non-finite values.
Results may differ from a plain program's by a relative error of at most 0.018.
Values may be sent and summed in bfloat16 or wider, within the bound.
A program may use at most 128 MiB of HBM per device.

v0:
```python
import jax
import jax.numpy as jnp
from jax import lax
from jax.sharding import PartitionSpec as P

HEADS = 16


def gelu_slope(pre):
    cdf = 0.5 * (1.0 + lax.erf(pre * 0.7071067811865476))
    pdf = jnp.exp(-0.5 * pre * pre) * 0.3989422804014327
    return cdf + pre * pdf


def contract_first(left, right):
    return lax.dot_general(
        left, right, (((0,), (0,)), ((), ())), preferred_element_type=jnp.float32
    )


def contract_last(left, right):
    return lax.dot_general(
        left, right, (((1,), (1,)), ((), ())), preferred_element_type=jnp.float32
    )


def body(
    tokens,
    queries,
    keys,
    values,
    ln_gain,
    mean_in,
    sigma_in,
    noise_in,
    mean_out,
    sigma_out,
    noise_out,
    flip_in,
    flip_mid,
    flip_hidden,
    flip_out,
    cotangent,
):
    bf = jnp.bfloat16
    f32 = jnp.float32
    own_images, patches, width = tokens.shape
    hidden_local = mean_in.shape[1]
    head_dim = width // HEADS
    scale = head_dim ** (-0.5)
    pert_in = (sigma_in.astype(f32) * noise_in.astype(f32)).astype(bf)
    pert_out = (sigma_out.astype(f32) * noise_out.astype(f32)).astype(bf)
    query_heads = queries.reshape(own_images, patches, HEADS, head_dim)
    key_heads = keys.reshape(own_images, patches, HEADS, head_dim)
    value_heads = values.reshape(own_images, patches, HEADS, head_dim)
    scores = (
        jnp.einsum("bqhe,bkhe->bhqk", query_heads, key_heads, preferred_element_type=f32) * scale
    )
    top = jnp.max(scores, axis=-1, keepdims=True)
    expd = jnp.exp(scores - top)
    total = jnp.sum(expd, axis=-1)
    accum = jnp.einsum("bhqk,bkhe->bqhe", expd.astype(bf), value_heads, preferred_element_type=f32)
    attn_out = (
        (accum / jnp.transpose(total, (0, 2, 1))[..., None])
        .reshape(own_images, patches, width)
        .astype(bf)
    )
    resid = (tokens.astype(f32) + attn_out.astype(f32)).astype(bf)
    resid_f = resid.astype(f32)
    centered = resid_f - jnp.mean(resid_f, axis=-1, keepdims=True)
    rstd = lax.rsqrt(jnp.mean(centered * centered, axis=-1, keepdims=True) + 1e-06)
    ahat = centered * rstd
    gain_f = ln_gain.astype(f32)
    normed = (ahat * gain_f).astype(bf)
    in_signs = flip_in.astype(bf)[:, None, :]
    in_signs_f = flip_in.astype(f32)[:, None, :]
    mid_signs = flip_mid.astype(bf)[:, None, :]
    mid_signs_f = flip_mid.astype(f32)[:, None, :]
    hid_signs = flip_hidden.astype(bf)[:, None, :]
    hid_signs_f = flip_hidden.astype(f32)[:, None, :]
    out_signs = flip_out.astype(bf)[:, None, :]
    out_signs_f = flip_out.astype(f32)[:, None, :]
    gathered = lax.all_gather(normed, "seq", axis=0, tiled=True)
    count = gathered.shape[0]
    signs = in_signs
    flat = gathered.reshape(-1, width)
    flat_flip = (gathered * signs).reshape(-1, width)
    plain = jnp.dot(flat, mean_in, preferred_element_type=f32).reshape(count, patches, hidden_local)
    noisy = jnp.dot(flat_flip, pert_in, preferred_element_type=f32).reshape(
        count, patches, hidden_local
    )
    pre = plain + noisy * mid_signs_f
    group_images = pre.shape[0]
    rows = group_images * patches
    hidden = jax.nn.gelu(pre, approximate=False).astype(bf)
    flipped_hidden = hidden * hid_signs
    count = lax.axis_size("seq") * own_images
    hb = hidden.reshape(-1, hidden_local)
    hfb = flipped_hidden.reshape(-1, hidden_local)
    plain = jnp.dot(hb, mean_out, preferred_element_type=f32).reshape(count, patches, width)
    noisy = jnp.dot(hfb, pert_out, preferred_element_type=f32).reshape(count, patches, width)
    mixed = lax.psum_scatter(
        (plain + noisy * out_signs_f).astype(jnp.bfloat16), "seq", scatter_dimension=0, tiled=True
    ).astype(jnp.float32)
    block_out = (resid_f + mixed).astype(bf)
    cot_all = lax.all_gather(cotangent, "seq", axis=0, tiled=True)
    cot_flat = cot_all.reshape(rows, width)
    cot_flip_flat = (cot_all * out_signs).reshape(rows, width)
    dhidden = contract_last(cot_flat, mean_out).reshape(group_images, patches, hidden_local)
    dhidden = (
        dhidden
        + contract_last(cot_flip_flat, pert_out).reshape(group_images, patches, hidden_local)
        * hid_signs_f
    )
    dpre = (dhidden * gelu_slope(pre)).astype(bf)
    dpre_flip = dpre * mid_signs
    local_mean_out = contract_first(hidden.reshape(rows, hidden_local), cot_flat)
    local_sigma_out = contract_first(
        flipped_hidden.reshape(rows, hidden_local), cot_flip_flat
    ) * noise_out.astype(f32)
    grad_mean_out, grad_sigma_out = (
        lax.psum(local_mean_out.astype(jnp.bfloat16), "dp").astype(jnp.float32),
        lax.psum(local_sigma_out.astype(jnp.bfloat16), "dp").astype(jnp.float32),
    )
    local_mean_in = contract_first(gathered.reshape(rows, width), dpre.reshape(rows, hidden_local))
    local_flip_in = contract_first(
        (gathered * in_signs).reshape(rows, width), dpre_flip.reshape(rows, hidden_local)
    )
    local_sigma_in = local_flip_in * noise_in.astype(f32)
    count = lax.axis_size("seq") * own_images
    drows = dpre.reshape(-1, hidden_local)
    dflip_rows = dpre_flip.reshape(-1, hidden_local)
    signs = in_signs_f
    plain = contract_last(drows, mean_in).reshape(count, patches, width)
    noisy = contract_last(dflip_rows, pert_in).reshape(count, patches, width)
    dnormed = lax.psum_scatter(
        (plain + noisy * signs).astype(jnp.bfloat16), "seq", scatter_dimension=0, tiled=True
    ).astype(jnp.float32)
    grad_mean_in, grad_sigma_in = (
        lax.psum(local_mean_in.astype(jnp.bfloat16), "dp").astype(jnp.float32),
        lax.psum(local_sigma_in.astype(jnp.bfloat16), "dp").astype(jnp.float32),
    )
    scaled = dnormed * gain_f
    back = rstd * (
        scaled
        - jnp.mean(scaled, axis=-1, keepdims=True)
        - ahat * jnp.mean(scaled * ahat, axis=-1, keepdims=True)
    )
    resid_grad = (cotangent.astype(f32) + back).astype(bf)
    return (block_out, resid_grad, grad_mean_in, grad_sigma_in, grad_mean_out, grad_sigma_out)


def solution(mesh):
    return jax.shard_map(
        body,
        mesh=mesh,
        in_specs=(
            P(("dp", "seq"), None, None),
            P(("dp", "seq"), None, None),
            P(("dp", "seq"), None, None),
            P(("dp", "seq"), None, None),
            P(),
            P(None, "seq"),
            P(None, "seq"),
            P(None, "seq"),
            P("seq", None),
            P("seq", None),
            P("seq", None),
            P("dp", None),
            P("dp", "seq"),
            P("dp", "seq"),
            P("dp", None),
            P(("dp", "seq"), None, None),
        ),
        out_specs=(
            P(("dp", "seq"), None, None),
            P(("dp", "seq"), None, None),
            P(None, "seq"),
            P(None, "seq"),
            P("seq", None),
            P("seq", None),
        ),
        check_vma=False,
    )
```

profile of v0, /device:TPU:0, one launch (start us, length us, event | category | flops | bytes accessed | tf_op | source)
XLA Modules:
  0.0 289.0 jit_solution(1723222755347720097)
XLA Ops:
  7.2 0.0 copy-start
  7.2 0.0 all-gather.3.cloned.1.call-start
  7.2 1.4 copy.42
  8.6 1.2 copy.40
  9.9 0.2 copy.41
  10.1 0.8 multiply_reduce_fusion
  10.8 0.7 fusion
  11.6 0.9 divide_convert_fusion
  12.5 0.1 bitcast_convert_fusion.2
  12.6 1.3 copy.44
  13.9 1.5 convert_reduce_fusion
  15.5 0.3 fusion.51
  15.8 1.1 fusion.45
  16.9 0.0 all-gather.3.cloned.1.call-update
  16.9 0.0 all-gather.5.cloned.1.call-start
  16.9 0.7 all-gather.5.cloned.1.call-update
  17.6 0.2 all-reduce.5.cloned.1.call-start
  18.0 37.0 %all-gather.3.cloned.1.call-done = bf16[4,256,1024]{2,1,0:T(8,128)(2,1)} async-done(((bf16[1,256,1024]{2,1,0:T(8,128)(2,1)}), bf16[4,256,1024]{2,1,0:T(8,128)(2,1)}) %all-gather.3.cloned.1.call-update) | async-done | bytes 2097168 | tf_op jit(solution)/shard_map/all_gather | solution.py:83
  55.0 3.3 %fusion.31 = f32[4,256,512]{2,1,0:T(8,128)S(1)} fusion(bf16[4,256,1024]{2,1,0:T(8,128)(2,1)} %all-gather.3.cloned.1.call-done, bf16[4,1024]{1,0:T(4,128)(2,1)S(1)} %get-tuple-element.19, bf16[1024,512]{1,0:T(8,128)(2,1)S(1)} %copy-done.7, bf16[1024,512]{1,0:T(8,128)(2,1)} %param.22), kind=kOutput, calls=%fused_computation.55 | convolution fusion | flops 1076887552 | bytes 6299648 | tf_op jit(solution)/shard_map/dot_general | solution.py:89
  58.3 1.9 fusion.77
  60.2 1.3 copy-done.4
  61.5 4.7 %fusion.8 = bf16[4,256,512]{2,1,0:T(8,128)(2,1)S(1)} fusion(f32[4,256,512]{2,1,0:T(8,128)S(1)} %get-tuple-element.28, u8[256,512]{1,0:T(8,128)(4,1)S(1)} %get-tuple-element.7, u8[256,512]{1,0:T(8,128)(4,1)S(1)} %get-tuple-element.6), kind=kLoop, calls=%fused_computation.18 | loop fusion | flops 36700160 | bytes 3407872 | tf_op jit(solution)/shard_map/convert_element_type | solution.py:95
  66.2 25.8 %all-gather.5.cloned.1.call-done = bf16[4,256,1024]{2,1,0:T(8,128)(2,1)} async-done(((bf16[1,256,1024]{2,1,0:T(8,128)(2,1)}), bf16[4,256,1024]{2,1,0:T(8,128)(2,1)}) %all-gather.5.cloned.1.call-update) | async-done | bytes 2097168 | tf_op jit(solution)/shard_map/all_gather | solution.py:106
  92.0 3.6 %fusion.27 = f32[4,256,512]{2,1,0:T(8,128)S(1)} fusion(bf16[4,256,1024]{2,1,0:T(8,128)(2,1)} %all-gather.5.cloned.1.call-done, bf16[4,1024]{1,0:T(4,128)(2,1)S(1)} %get-tuple-element.20, bf16[512,1024]{1,0:T(8,128)(2,1)} %param.26, bf16[512,1024]{1,0:T(8,128)(2,1)} %param.25), kind=kOutput, calls=%fused_computation.51 | convolution fusion | flops 1076887552 | bytes 6299648 | tf_op jit(solution)/shard_map/dot_general | solution.py:22
  95.7 0.1 copy-done.17
  95.8 2.0 fusion.14
  97.8 2.3 bitcast_convert_fusion.1
  100.1 2.3 fusion.3
  102.4 2.3 bitcast_convert_fusion
  104.6 2.4 fusion.5
  107.0 0.0 all-reduce.5.cloned.1.call-update
  107.0 0.3 reduce-scatter.9.cloned.1.call-start
  107.3 2.7 fusion.58
  110.0 2.6 add_convert_fusion
  112.6 0.0 reduce-scatter.9.cloned.1.call-update
  112.7 0.0 reduce-scatter.7.cloned.1.call-start
  112.7 2.6 fusion.56
  115.4 2.6 add_convert_fusion.1
  118.0 0.0 reduce-scatter.7.cloned.1.call-update
  118.0 85.7 %all-reduce.5.cloned.1.call-done = (bf16[1024,512]{1,0:T(8,128)(2,1)}, bf16[1024,512]{1,0:T(8,128)(2,1)}, bf16[512,1024]{1,0:T(8,128)(2,1)}, bf16[512,1024]{1,0:T(8,128)(2,1)}) async-done(((bf16[1024,512]{1,0:T(8,128)(2,1)}, bf16[1024,512]{1,0:T(8,128)(2,1)}, bf16[512,1024]{1,0:T(8,128)(2,1)}, bf16[512,1024]{1,0:T(8,128)(2,1)}), (bf16[1024,512]{1,0:T(8,128)(2,1)}, bf16[1024,512]{1,0:T(8,128)(2,1)}, ...) | async-done | bytes 4194320 | tf_op jit(solution)/shard_map/psum | solution.py:140
  203.7 2.9 %convert_element_type.173 = f32[1024,512]{1,0:T(8,128)} convert(bf16[1024,512]{1,0:T(8,128)(2,1)} %get-tuple-element.10) | non-fusion elementwise | flops 524288 | bytes 3145728 | tf_op jit(solution)/shard_map/convert_element_type | solution.py:140
  206.7 1.6 convert_element_type.175
  208.3 1.6 convert_element_type.177
  209.8 1.6 convert_element_type.179
  211.4 30.4 %reduce-scatter.9.cloned.1.call-done = bf16[1,256,1024]{2,1,0:T(8,128)(2,1)} async-done(((bf16[4,256,1024]{2,1,0:T(8,128)(2,1)}), bf16[1,256,1024]{2,1,0:T(8,128)(2,1)}) %reduce-scatter.9.cloned.1.call-update) | async-done | bytes 524304
  241.8 1.4 fusion.61
  243.2 36.6 %reduce-scatter.7.cloned.1.call-done = bf16[1,256,1024]{2,1,0:T(8,128)(2,1)} async-done(((bf16[4,256,1024]{2,1,0:T(8,128)(2,1)}), bf16[1,256,1024]{2,1,0:T(8,128)(2,1)}) %reduce-scatter.7.cloned.1.call-update) | async-done | bytes 524304
  279.8 2.6 fusion.50
  (59 shorter events, 0.2 us)
Async XLA Ops:
  7.2 51.1 %copy-start = (bf16[1024,512]{1,0:T(8,128)(2,1)S(1)}, bf16[1024,512]{1,0:T(8,128)(2,1)}, u32[]{:S(2)}) copy-start(bf16[1024,512]{1,0:T(8,128)(2,1)} %param.21) | copy-start | bytes 3145732
  7.2 2.7 copy-start.18
  7.2 47.8 %all-gather.3.cloned.1.call-start = ((), (), s32[]{:S(2)}) async-start(), calls=%async_computation.2 | async-start | bytes 2621440 | tf_op jit(solution)/shard_map/all_gather | solution.py:83
  12.4 1.4 copy-start.24
  12.4 1.4 copy-start.19
  13.9 4.0 %copy-start.22 = (s32[4,512]{1,0:T(4,128)S(1)}, s32[4,512]{1,0:T(4,128)}, u32[]{:S(2)}) copy-start(s32[4,512]{1,0:T(4,128)} %param.28) | copy-start | bytes 24580
  13.9 4.0 %copy-start.23 = (s32[4,512]{1,0:T(4,128)S(1)}, s32[4,512]{1,0:T(4,128)}, u32[]{:S(2)}) copy-start(s32[4,512]{1,0:T(4,128)} %param.29) | copy-start | bytes 24580
  13.9 4.0 %copy-start.20 = (s32[4,1024]{1,0:T(4,128)S(1)}, s32[4,1024]{1,0:T(4,128)}, u32[]{:S(2)}) copy-start(s32[4,1024]{1,0:T(4,128)} %param.27) | copy-start | bytes 49156
  13.9 4.0 %copy-start.21 = (s32[4,1024]{1,0:T(4,128)S(1)}, s32[4,1024]{1,0:T(4,128)}, u32[]{:S(2)}) copy-start(s32[4,1024]{1,0:T(4,128)} %param.30) | copy-start | bytes 49156
  13.9 41.0 %copy-start.7 = (bf16[1024,512]{1,0:T(8,128)(2,1)S(1)}, bf16[1024,512]{1,0:T(8,128)(2,1)}, u32[]{:S(2)}) copy-start(bf16[1024,512]{1,0:T(8,128)(2,1)} %param.23) | copy-start | bytes 3145732
  16.9 75.1 %all-gather.5.cloned.1.call-start = ((), (), s32[]{:S(2)}) async-start(), calls=%async_computation.3 | async-start | bytes 2621440 | tf_op jit(solution)/shard_map/all_gather | solution.py:106
  17.6 186.1 %all-reduce.5.cloned.1.call-start = ((), (), s32[]{:S(2)}) async-start(), calls=%async_computation.6 | async-start | bytes 8388608 | tf_op jit(solution)/shard_map/psum | solution.py:140
  55.0 3.3 %copy-start.25 = (bf16[4,256,1024]{2,1,0:T(8,128)(2,1)S(1)}, bf16[4,256,1024]{2,1,0:T(8,128)(2,1)}, u32[]{:S(2)}) copy-start(bf16[4,256,1024]{2,1,0:T(8,128)(2,1)} %all-gather.3.cloned.1.call-done) | copy-start | bytes 6291460
  60.2 1.3 copy-start.4
  92.0 3.6 %copy-start.3 = (bf16[4,256,1024]{2,1,0:T(8,128)(2,1)S(1)}, bf16[4,256,1024]{2,1,0:T(8,128)(2,1)}, u32[]{:S(2)}) copy-start(bf16[4,256,1024]{2,1,0:T(8,128)(2,1)} %all-gather.5.cloned.1.call-done) | copy-start | bytes 6291460
  92.0 3.6 %copy-start.5 = (f32[4,256,512]{2,1,0:T(8,128)S(1)}, f32[4,256,512]{2,1,0:T(8,128)}, u32[]{:S(2)}) copy-start(f32[4,256,512]{2,1,0:T(8,128)} %copy-done.4) | copy-start | bytes 6291460
  92.0 3.7 %copy-start.17 = (bf16[512,1024]{1,0:T(8,128)(2,1)S(1)}, bf16[512,1024]{1,0:T(8,128)(2,1)}, u32[]{:S(2)}) copy-start(bf16[512,1024]{1,0:T(8,128)(2,1)} %param.24) | copy-start | bytes 3145732
  95.8 2.1 copy-start.26
  97.8 2.3 copy-start.1
  97.8 2.3 copy-start.8
  102.4 2.3 copy-start.11
  107.0 134.8 %reduce-scatter.9.cloned.1.call-start = ((), (), s32[]{:S(2)}) async-start(), calls=%async_computation.5 | async-start | bytes 2621440
  107.3 2.7 copy-start.2
  107.3 2.7 copy-start.9
  107.3 2.7 copy-start.10
  112.7 167.2 %reduce-scatter.7.cloned.1.call-start = ((), (), s32[]{:S(2)}) async-start(), calls=%async_computation.4 | async-start | bytes 2621440
  112.7 2.7 copy-start.12
  112.7 2.7 copy-start.13
  203.7 2.9 %copy-start.16 = (bf16[1024,512]{1,0:T(8,128)(2,1)S(1)}, bf16[1024,512]{1,0:T(8,128)(2,1)}, u32[]{:S(2)}) copy-start(bf16[1024,512]{1,0:T(8,128)(2,1)} %get-tuple-element.11) | copy-start | bytes 3145732
  206.6 1.6 copy-start.15
  208.3 1.6 copy-start.14
  209.8 70.0 %copy-start.6 = (bf16[1,256,1024]{2,1,0:T(8,128)(2,1)S(1)}, bf16[1,256,1024]{2,1,0:T(8,128)(2,1)}, u32[]{:S(2)}) copy-start(bf16[1,256,1024]{2,1,0:T(8,128)(2,1)} %param.31) | copy-start | bytes 1572868
Sparse Core Ops, SparseCore 0:
  17.0 37.8 all-gather.2
  56.8 35.1 all-gather.4
  107.1 96.5 all-reduce.4
  206.5 35.2 reduce-scatter.8
  244.6 35.1 reduce-scatter.6
where the time goes:
time: 289 us
  waiting for transfers between devices  216 us (75%)
  matrix products  32.2 us (11%)
  other arithmetic  20.2 us (7%)
  between operations  14.2 us (5%)
  local copies, waits for them, and re-layouts  5.66 us (2%)
    psum x1, waiting for transfers between devices, body(): lax.psum(local_mean_in.astype(jnp.bfloat16), 'dp').astype(jnp.float32)  85.7 us
    unnamed x7, waiting for transfers between devices  67.8 us
    all_gather x1, waiting for transfers between devices, body(): gathered = lax.all_gather(normed, 'seq', axis=0, tiled=True)  37 us
    all_gather x1, waiting for transfers between devices, body(): cot_all = lax.all_gather(cotangent, 'seq', axis=0, tiled=True)  25.8 us
    dot_general x4, matrix products, contract_last(): lax.dot_general(left, right, (((1,), (1,)), ((), ())), preferred_element_...  11 us
    dot_general x4, matrix products, contract_first(): lax.dot_general(left, right, (((0,), (0,)), ((), ())), preferred_element_...  9.14 us
  transfers between devices with their start and end apart: 5, of which 5 were waited for; matrix products, arithmetic and copies ran while one was open for 10% of the time, Pallas kernels for 0%

commit v1 on v0

v1 whole, which is shorter than its diff:
```python
import functools
import math

import jax
import jax.numpy as jnp
from jax import lax
from jax.experimental import pallas as pl
from jax.experimental.pallas import tpu as pltpu
from jax.sharding import PartitionSpec as P

HEADS = 16
LANES = 128
CORES = 2
BF = jnp.bfloat16
F32 = jnp.float32
MESH = pl.DeviceIdType.MESH


def piece_shape(rows, cols, dp):
    if (rows // dp) % 16 == 0:
        return rows // dp, cols
    return rows * CORES // dp, cols // CORES


def dot_last(left, right):
    return lax.dot_general(left, right, (((1,), (1,)), ((), ())), preferred_element_type=F32)


def dot_first(left, right):
    return lax.dot_general(left, right, (((0,), (0,)), ((), ())), preferred_element_type=F32)


def dot(left, right):
    return jnp.dot(left, right, preferred_element_type=F32)


def norm_stats(resid_f):
    centered = resid_f - jnp.mean(resid_f, axis=-1, keepdims=True)
    rstd = lax.rsqrt(jnp.mean(centered * centered, axis=-1, keepdims=True) + 1e-06)
    return centered * rstd, rstd


def kernel(
    dp,
    seq,
    tok, que, key, val, gain, mean_in, sig_in, noi_in, mean_out, sig_out, noi_out,
    f_in, f_mid, f_hid, f_out, cot,
    out_block, out_grad, o_mo, o_so, o_mi, o_si,
    pert_in, pert_out, resid, cot_all, nrm_all, hid, hid_f, dpre, dpre_f,
    own, part_m, part_d, got_m, got_d,
    pieces, pairs, ups, downs, fulls,
    cot_s, cot_r, nrm_s, nrm_r, mix_s, mix_r, dnr_s, dnr_r,
    pair_s, pair_r, up_s, up_r, dn_s, dn_r, gu_s, gu_r, gd_s, gd_r, gp_s, gp_r, out_sem,
):
    my_dp = lax.axis_index("dp")
    me = lax.axis_index("seq")
    nz = dp // CORES
    z = my_dp // CORES
    core = my_dp % CORES
    partner = (z * CORES + (1 - core), me)
    above = (my_dp + CORES, me)
    below = (my_dp - CORES, me)
    base = math.isqrt(seq)
    if base * base != seq:
        base = seq
    tall = seq // base
    slots = part_m.shape[0]
    patches, width = resid.shape
    head_dim = width // HEADS
    scale = head_dim ** (-0.5)

    def shifted(k, sign):
        row = (me // base + sign * (k // base) + tall) % tall
        return row * base + (me % base + sign * (k % base) + base) % base

    def remote(src, dst, s, r, dev):
        return pltpu.make_async_remote_copy(
            src_ref=src, dst_ref=dst, send_sem=s, recv_sem=r, device_id=dev, device_id_type=MESH
        )

    def peer(index):
        return (my_dp, index)

    barrier = pltpu.get_barrier_semaphore()

    def greet(dev):
        pl.semaphore_signal(barrier, inc=1, device_id=dev, device_id_type=MESH)

    for k in range(1, seq):
        greet(peer(shifted(k, 1)))
    greet(partner)

    @pl.when(z > 0)
    def _():
        greet(below)

    @pl.when(z < nz - 1)
    def _():
        greet(above)

    chained = (z + nz - 1) // nz + (nz - 1 - z + nz - 1) // nz
    pl.semaphore_wait(barrier, seq + chained)

    def cot_copy(k):
        return remote(cot.at[0], cot_all.at[me], cot_s.at[k], cot_r.at[me], peer(shifted(k, 1)))

    def nrm_copy(k):
        return remote(
            nrm_all.at[me], nrm_all.at[me], nrm_s.at[k], nrm_r.at[me], peer(shifted(k, 1))
        )

    for k in range(1, seq):
        cot_copy(k).start()

    group = LANES // head_dim
    lane = lax.broadcasted_iota(jnp.int32, (1, LANES), 1)
    masks = [
        jnp.where((lane >= h * head_dim) & (lane < (h + 1) * head_dim), 1.0, 0.0).astype(F32)
        for h in range(group)
    ]

    def heads(p, carry):
        cols = pl.ds(pl.multiple_of(p * LANES, LANES), LANES)
        q, kk, v = que[0, :, cols], key[0, :, cols], val[0, :, cols]
        acc = jnp.zeros((patches, LANES), F32)
        for mask in masks:
            scores = dot_last(q * mask.astype(BF), kk) * scale
            expd = jnp.exp(scores - jnp.max(scores, axis=-1, keepdims=True))
            total = jnp.sum(expd, axis=-1, keepdims=True)
            acc = acc + (dot(expd.astype(BF), v) / total) * mask
        attn = acc.astype(BF).astype(F32)
        resid[:, cols] = (tok[0, :, cols].astype(F32) + attn).astype(BF)
        return carry

    lax.fori_loop(0, width // LANES, heads, 0)
    gain_f = gain[...].astype(F32)
    ahat, _ = norm_stats(resid[...].astype(F32))
    nrm_all[me] = (ahat * gain_f).astype(BF)
    for k in range(1, seq):
        nrm_copy(k).start()

    pert_in[...] = (sig_in[...].astype(F32) * noi_in[...].astype(F32)).astype(BF)
    pert_out[...] = (sig_out[...].astype(F32) * noi_out[...].astype(F32)).astype(BF)
    cot_all[me] = cot[0]

    def mix_copy(k, j):
        slot = (k - 1) % slots
        return remote(part_m.at[slot], got_m.at[me], mix_s.at[slot], mix_r.at[me], peer(j))

    def dnr_copy(k, j):
        slot = (k - 1) % slots
        return remote(part_d.at[slot], got_d.at[me], dnr_s.at[slot], dnr_r.at[me], peer(j))

    def arrived(dst, sem):
        remote(dst, dst, sem, sem, peer(me)).wait_recv()

    def signs(ref, j):
        return ref[pl.ds(j, 1), :].astype(F32)

    def block(k, first):
        j = me if first else shifted(k, -1)
        s_in, s_mid, s_hid, s_out = signs(f_in, j), signs(f_mid, j), signs(f_hid, j), signs(f_out, j)
        if not first:
            arrived(nrm_all.at[j], nrm_r.at[j])
        x = nrm_all[j]
        pre = dot(x, mean_in[...]) + dot(x * s_in.astype(BF), pert_in[...]) * s_mid
        cdf = 0.5 * (1.0 + lax.erf(pre * 0.7071067811865476))
        slope = cdf + pre * (jnp.exp(-0.5 * pre * pre) * 0.3989422804014327)
        h = (pre * cdf).astype(BF)
        hf = h * s_hid.astype(BF)
        hid[j] = h
        hid_f[j] = hf
        mixed = (dot(h, mean_out[...]) + dot(hf, pert_out[...]) * s_out).astype(BF)
        if first:
            own[0] = mixed
        else:
            @pl.when(k > slots)
            def _():
                mix_copy(k, j).wait_send()
                dnr_copy(k, j).wait_send()

            part_m[(k - 1) % slots] = mixed
            mix_copy(k, j).start()
            arrived(cot_all.at[j], cot_r.at[j])
        c = cot_all[j]
        dh = dot_last(c, mean_out[...]) + dot_last(c * s_out.astype(BF), pert_out[...]) * s_hid
        d = (dh * slope).astype(BF)
        df = d * s_mid.astype(BF)
        dpre[j] = d
        dpre_f[j] = df
        dn = (dot_last(d, mean_in[...]) + dot_last(df, pert_in[...]) * s_in).astype(BF)
        if first:
            own[1] = dn
        else:
            part_d[(k - 1) % slots] = dn
            dnr_copy(k, j).start()

    block(0, True)

    def step(k, carry):
        block(k, False)
        return carry

    lax.fori_loop(1, seq, step, 0)

    rows = seq * patches

    def produce(a, left, right):
        total_rows, cols = left.shape[2], right.shape[2]
        _, _, pr, pc = pieces[a].shape
        tile = min(256, total_rows)
        rhs = right[...].reshape(rows, cols)
        for t in range(total_rows // tile):
            lhs = left[:, :, t * tile : (t + 1) * tile].reshape(rows, tile)
            g = dot_first(lhs, rhs).astype(BF)
            for c in range(CORES):
                for s in range(nz):
                    lo = (c * nz + s) * pr if pc == cols else s * pr
                    left_col = 0 if pc == cols else c * pc
                    if t * tile <= lo < (t + 1) * tile:
                        pieces[a][c, s] = g[lo - t * tile : lo - t * tile + pr, left_col : left_col + pc]
        pair_copy(a).start()

    def pair_copy(a):
        return remote(pieces[a].at[1 - core], pairs[a], pair_s.at[a], pair_r.at[a], partner)

    def up_copy(a, d, src):
        return remote(src, ups[a].at[d], up_s.at[a, d], up_r.at[a, d], above)

    def down_copy(a, d, src):
        return remote(src, downs[a].at[d], dn_s.at[a, d], dn_r.at[a, d], below)

    def merge(a):
        arrived(pairs[a], pair_r.at[a])
        pairs[a][...] = (pairs[a][...].astype(F32) + pieces[a][core].astype(F32)).astype(BF)

        @pl.when(z == 0)
        def _():
            for d in range(nz - 1, 0, -1):
                up_copy(a, d, pairs[a].at[d]).start()

        @pl.when(z == nz - 1)
        def _():
            for d in range(nz - 1):
                down_copy(a, d, pairs[a].at[d]).start()

    def chain(a):
        for i in range(nz):
            d = nz - 1 - i

            @pl.when((z > 0) & (z < d))
            def _():
                arrived(ups[a].at[d], up_r.at[a, d])
                ups[a][d] = (ups[a][d].astype(F32) + pairs[a][d].astype(F32)).astype(BF)
                up_copy(a, d, ups[a].at[d]).start()

            @pl.when((z < nz - 1) & (z > i))
            def _():
                arrived(downs[a].at[i], dn_r.at[a, i])
                downs[a][i] = (downs[a][i].astype(F32) + pairs[a][i].astype(F32)).astype(BF)
                down_copy(a, i, downs[a].at[i]).start()

    def hand_up(a, d):
        return remote(fulls[a].at[core, d], fulls[a].at[core, d], gu_s.at[a, d], gu_r.at[a, d], above)

    def hand_down(a, d):
        return remote(fulls[a].at[core, d], fulls[a].at[core, d], gd_s.at[a, d], gd_r.at[a, d], below)

    def hand_over(a, d):
        return remote(fulls[a].at[core, d], fulls[a].at[core, d], gp_s.at[a, d], gp_r.at[a, d], partner)

    def finish(a):
        for d in range(nz):
            @pl.when(z == d)
            def _():
                total = pairs[a][d].astype(F32)
                if d > 0:
                    arrived(ups[a].at[d], up_r.at[a, d])
                    total = total + ups[a][d].astype(F32)
                if d < nz - 1:
                    arrived(downs[a].at[d], dn_r.at[a, d])
                    total = total + downs[a][d].astype(F32)
                fulls[a][core, d] = total.astype(BF)
                if d < nz - 1:
                    hand_up(a, d).start()
                if d > 0:
                    hand_down(a, d).start()
                hand_over(a, d).start()

    def spread(a):
        for i in range(1, nz):
            low, high = z - i, z + i

            @pl.when(low >= 0)
            def _():
                arrived(fulls[a].at[core, low], gu_r.at[a, low])

                @pl.when(z < nz - 1)
                def _():
                    hand_up(a, low).start()

                hand_over(a, low).start()

            @pl.when(high < nz)
            def _():
                arrived(fulls[a].at[core, high], gd_r.at[a, high])

                @pl.when(z > 0)
                def _():
                    hand_down(a, high).start()

                hand_over(a, high).start()

    produce(0, hid, cot_all)
    produce(2, nrm_all, dpre)
    merge(0)
    for k in range(1, seq):
        nrm_copy(k).wait_send()
    cot_all[...] = cot_all[...] * f_out[...].astype(F32).astype(BF)[:, None, :]
    produce(1, hid_f, cot_all)
    chain(0)
    merge(2)
    nrm_all[...] = nrm_all[...] * f_in[...].astype(F32).astype(BF)[:, None, :]
    produce(3, nrm_all, dpre_f)
    merge(1)
    merge(3)
    chain(2)
    finish(0)
    chain(1)
    finish(2)
    spread(0)
    chain(3)
    finish(1)
    spread(2)
    finish(3)
    spread(1)

    def gather_sum(slot, buf, sem):
        total = own[slot].astype(F32)
        for k in range(1, seq):
            j = shifted(k, -1)
            arrived(buf.at[j], sem.at[j])
            total = total + buf[j].astype(F32)
        return total

    resid_f = resid[...].astype(F32)
    out_block[0] = (resid_f + gather_sum(0, got_m, mix_r)).astype(BF)
    scaled = gather_sum(1, got_d, dnr_r) * gain_f
    ahat, rstd = norm_stats(resid_f)
    back = rstd * (
        scaled
        - jnp.mean(scaled, axis=-1, keepdims=True)
        - ahat * jnp.mean(scaled * ahat, axis=-1, keepdims=True)
    )
    out_grad[0] = (cot[0].astype(F32) + back).astype(BF)
    spread(3)

    outs = (o_mo, o_so, o_mi, o_si)

    def drain(a):
        for d in range(nz):
            arrived(fulls[a].at[1 - core, d], gp_r.at[a, d])
        pltpu.make_async_copy(fulls[a], outs[a], out_sem.at[a]).start()

    for a in range(4):
        drain(a)

    for k in range(1, seq):
        cot_copy(k).wait_send()
    for k in range(max(1, seq - slots), seq):
        mix_copy(k, me).wait_send()
        dnr_copy(k, me).wait_send()
    for a in range(4):
        pair_copy(a).wait_send()
        for d in range(nz):
            @pl.when((z < d) & (z < nz - 1))
            def _():
                up_copy(a, d, ups[a].at[d]).wait_send()

            @pl.when((z > d) & (z > 0))
            def _():
                down_copy(a, d, downs[a].at[d]).wait_send()

            @pl.when((z >= d) & (z < nz - 1))
            def _():
                hand_up(a, d).wait_send()

            @pl.when((z <= d) & (z > 0))
            def _():
                hand_down(a, d).wait_send()

            hand_over(a, d).wait_send()
    for a in range(4):
        pltpu.make_async_copy(fulls[a], outs[a], out_sem.at[a]).wait()


def body(dp, seq, *args):
    tokens, mean_in, mean_out = args[0], args[5], args[8]
    noise_in, noise_out = args[7], args[10]
    own, patches, width = tokens.shape
    assert own == 1
    hidden = mean_in.shape[1]
    nz = dp // CORES
    shapes = [(hidden, width)] * 2 + [(width, hidden)] * 2
    cut = [piece_shape(r, c, dp) for r, c in shapes]
    slots = max(1, min(seq - 1, 4))
    args = list(args)
    args[4] = args[4].reshape(1, width)
    vm = pltpu.VMEM
    tokens_all = (seq, patches, width)
    hidden_all = (seq, patches, hidden)
    dma = pltpu.SemaphoreType.DMA
    full = [(CORES, nz) + c for c in cut]
    scratch = [
        vm(mean_in.shape, BF),
        vm(mean_out.shape, BF),
        vm((patches, width), BF),
        vm(tokens_all, BF),
        vm(tokens_all, BF),
        *[vm(hidden_all, BF) for _ in range(4)],
        vm((2, patches, width), BF),
        vm((slots, patches, width), BF),
        vm((slots, patches, width), BF),
        vm(tokens_all, BF),
        vm(tokens_all, BF),
        [vm(f, BF) for f in full],
        *[[vm(f[1:], BF) for f in full] for _ in range(3)],
        [vm(f, BF) for f in full],
        *[dma((seq,)) for _ in range(4)],
        dma((slots,)), dma((seq,)), dma((slots,)), dma((seq,)),
        dma((4,)), dma((4,)),
        *[dma((4, nz)) for _ in range(10)],
        dma((4,)),
    ]
    whole = pl.BlockSpec(memory_space=pltpu.VMEM)
    away = pl.BlockSpec(memory_space=pl.ANY)
    res = pl.pallas_call(
        functools.partial(kernel, dp, seq),
        out_shape=[jax.ShapeDtypeStruct(tokens.shape, BF)] * 2
        + [jax.ShapeDtypeStruct(f, BF) for f in full],
        in_specs=[whole] * 16,
        out_specs=[whole, whole] + [away] * 4,
        scratch_shapes=scratch,
        compiler_params=pltpu.CompilerParams(
            collective_id=0, has_side_effects=True, vmem_limit_bytes=60 * 1024 * 1024
        ),
    )(*args)

    def assemble(a):
        r, c = shapes[a]
        g = res[2 + a]
        if cut[a][1] != c:
            g = jnp.transpose(g, (1, 2, 0, 3))
        return g.reshape(r, c).astype(F32)

    return (
        res[0],
        res[1],
        assemble(2),
        assemble(3) * noise_in.astype(F32),
        assemble(0),
        assemble(1) * noise_out.astype(F32),
    )


def solution(mesh):
    dp, seq = mesh.shape["dp"], mesh.shape["seq"]
    images = P(("dp", "seq"), None, None)
    cols, rows = P(None, "seq"), P("seq", None)
    return jax.shard_map(
        functools.partial(body, dp, seq),
        mesh=mesh,
        in_specs=(
            images, images, images, images, P(),
            cols, cols, cols, rows, rows, rows,
            P("dp", None), P("dp", "seq"), P("dp", "seq"), P("dp", None),
            images,
        ),
        out_specs=(images, images, cols, cols, rows, rows),
        check_vma=False,
    )
```

time: 289 us -> 164 us (0.57)
  waiting for transfers between devices: 216 us -> 0 us
  Pallas kernels: 0 us -> 152 us
  matrix products: 32.2 us -> 0 us
  between operations: 14.2 us -> 0.67 us
  other arithmetic: 20.2 us -> 8.09 us
    pallas_call x0 -> x1, Pallas kernels: none -> 152 us  [body(): pl.pallas_call(functools.partial(kernel, dp, seq), out_shape=[jax.ShapeDt...]
    psum x1 -> x0, waiting for transfers between devices: 85.7 us -> none  [body(): lax.psum(local_mean_in.astype(jnp.bfloat16), 'dp').astype(jnp.float32)]
    unnamed x7 -> x0, waiting for transfers between devices: 67.8 us -> none
    all_gather x2 -> x0, waiting for transfers between devices: 62.7 us -> none  [the longest x1 37 us: body(): gathered = lax.all_gather(normed, 'seq', axis=0, tiled=True)]
    dot_general x14 -> x0, matrix products: 32.2 us -> none  [the longest x4 11 us: contract_last(): lax.dot_general(left, right, (((1,), (1,)), ((), ())), preferred_element_...]
    convert_element_type x13 -> x2, other arithmetic: 16.2 us -> 4.61 us  [assemble(): return g.reshape(r, c).astype(F32)]
    reduce_sum x4 -> x0, other arithmetic: 3.92 us -> none  [the longest x1 1.51 us: body(): centered = resid_f - jnp.mean(resid_f, axis=-1, keepdims=True)]
    mul x0 -> x2, other arithmetic: none -> 3.48 us  [the longest x1 1.76 us: body(): assemble(1) * noise_out.astype(F32)]
  transfers between devices with their start and end apart: 5 -> 0, of which waited for: 5 -> 0; matrix products, arithmetic and copies ran while one was open for 10% -> 0% of each run, Pallas kernels for 0% -> 0%
where the time goes in v1:
time: 164 us
  Pallas kernels  152 us (93%)
  other arithmetic  8.09 us (5%)
  local copies, waits for them, and re-layouts  3.53 us (2%)
    pallas_call x1, Pallas kernels, body(): pl.pallas_call(functools.partial(kernel, dp, seq), out_shape=[jax.ShapeDt...  152 us
    convert_element_type x2, other arithmetic, assemble(): return g.reshape(r, c).astype(F32)  4.61 us

profile of v1, /device:TPU:0, one launch (start us, length us, event | category | flops | bytes accessed | tf_op | source)
XLA Modules:
  0.0 164.2 jit_solution(7008800865038480909)
XLA Ops:
  0.6 1.3 reshape.27.gain
  1.9 151.9 %shard_map.199 = (bf16[1,256,1024]{2,1,0:T(8,128)(2,1)}, bf16[1,256,1024]{2,1,0:T(8,128)(2,1)}, bf16[2,4,64,1024]{3,2,1,0:T(8,128)(2,1)}, bf16[2,4,64,1024]{3,2,...) custom-call(bf16[1,256,1024]{2,1,0:T(8,128)(2,1)} %tok.1, ...), custom_call_target="tpu_custom_call" | custom-call | tf_op jit(solution)/shard_map/pallas_call | solution.py:437
  153.8 0.0 copy-start
  153.8 0.0 copy-start.4
  153.8 3.0 %bitcast_convert_fusion.1 = f32[1024,512]{1,0:T(8,128)} fusion(bf16[2,4,128,512]{3,2,1,0:T(8,128)(2,1)} %get-tuple-element.14), kind=kLoop, calls=%fused_computation.3 | loop fusion | flops 524288 | bytes 3145728 | tf_op jit(solution)/shard_map/convert_element_type | solution.py:454
  156.8 0.0 copy-done
  156.8 0.0 copy-done.4
  156.8 0.0 copy-start.2
  156.8 1.7 %convert_multiply_fusion.1 = f32[1024,512]{1,0:T(8,128)} fusion(bf16[1024,512]{1,0:T(8,128)(2,1)S(1)} %copy-done, bf16[2,4,128,512]{3,2,1,0:T(8,128)(2,1)S(1)} %copy-done.4), kind=kLoop, calls=%fused_computation.1 | loop fusion | flops 1572864 | bytes 4194304 | tf_op jit(solution)/shard_map/mul | solution.py:460
  158.5 0.0 copy-done.2
  158.5 0.0 copy-start.1
  158.5 0.0 copy-start.3
  158.5 1.6 bitcast_convert_fusion
  160.2 0.0 copy-done.1
  160.2 0.6 copy-done.3
  160.8 0.0 copy-start.6
  160.8 0.0 copy-start.5
  160.8 1.8 %convert_multiply_fusion = f32[512,1024]{1,0:T(8,128)} fusion(bf16[512,1024]{1,0:T(8,128)(2,1)S(1)} %copy-done.1, bf16[2,4,64,1024]{3,2,1,0:T(8,128)(2,1)S(1)} %copy-done.3), kind=kLoop, calls=%fused_computation | loop fusion | flops 1572864 | bytes 4194304 | tf_op jit(solution)/shard_map/mul | solution.py:462
  162.6 0.0 copy-done.6
  162.6 0.8 copy.24
  163.4 0.0 copy-done.5
  163.4 0.8 copy.25
Async XLA Ops:
  153.8 3.0 %copy-start = (bf16[1024,512]{1,0:T(8,128)(2,1)S(1)}, bf16[1024,512]{1,0:T(8,128)(2,1)}, u32[]{:S(2)}) copy-start(bf16[1024,512]{1,0:T(8,128)(2,1)} %noi_in.1) | copy-start | bytes 3145732
  153.8 3.0 %copy-start.4 = (bf16[2,4,128,512]{3,2,1,0:T(8,128)(2,1)S(1)}, bf16[2,4,128,512]{3,2,1,0:T(8,128)(2,1)}, u32[]{:S(2)}) copy-start(bf16[2,4,128,512]{3,2,1,0:T(8,128)(2,1)} %get-tuple-element.15) | copy-start | bytes 3145732
  156.8 1.7 %copy-start.2 = (bf16[2,4,64,1024]{3,2,1,0:T(8,128)(2,1)S(1)}, bf16[2,4,64,1024]{3,2,1,0:T(8,128)(2,1)}, u32[]{:S(2)}) copy-start(bf16[2,4,64,1024]{3,2,1,0:T(8,128)(2,1)} %get-tuple-element.16) | copy-start | bytes 3145732
  158.5 1.6 copy-start.1
  158.5 2.3 %copy-start.3 = (bf16[2,4,64,1024]{3,2,1,0:T(8,128)(2,1)S(1)}, bf16[2,4,64,1024]{3,2,1,0:T(8,128)(2,1)}, u32[]{:S(2)}) copy-start(bf16[2,4,64,1024]{3,2,1,0:T(8,128)(2,1)} %get-tuple-element.17) | copy-start | bytes 3145732
  160.8 1.8 %copy-start.6 = (bf16[1,256,1024]{2,1,0:T(8,128)(2,1)S(1)}, bf16[1,256,1024]{2,1,0:T(8,128)(2,1)}, u32[]{:S(2)}) copy-start(bf16[1,256,1024]{2,1,0:T(8,128)(2,1)} %get-tuple-element.24) | copy-start | bytes 1572868
  160.8 2.6 %copy-start.5 = (bf16[1,256,1024]{2,1,0:T(8,128)(2,1)S(1)}, bf16[1,256,1024]{2,1,0:T(8,128)(2,1)}, u32[]{:S(2)}) copy-start(bf16[1,256,1024]{2,1,0:T(8,128)(2,1)} %get-tuple-element.25) | copy-start | bytes 1572868

commit v2 on v1

--- a/solution.py
+++ b/solution.py
@@ -43,14 +43,16 @@
 def kernel(
     dp,
     seq,
-    tok, que, key, val, gain, mean_in, sig_in, noi_in, mean_out, sig_out, noi_out,
+    tok, que, key, val, gain, h_mi, h_si, h_ni, h_mo, h_so, h_no,
     f_in, f_mid, f_hid, f_out, cot,
     out_block, out_grad, o_mo, o_so, o_mi, o_si,
+    mean_in, sig_in, noi_in, mean_out, sig_out, noi_out,
     pert_in, pert_out, resid, cot_all, nrm_all, hid, hid_f, dpre, dpre_f,
     own, part_m, part_d, got_m, got_d,
     pieces, pairs, ups, downs, fulls,
     cot_s, cot_r, nrm_s, nrm_r, mix_s, mix_r, dnr_s, dnr_r,
     pair_s, pair_r, up_s, up_r, dn_s, dn_r, gu_s, gu_r, gd_s, gd_r, gp_s, gp_r, out_sem,
+    cf_s, cf_r, nf_s, nf_r, load_sem,
 ):
     my_dp = lax.axis_index("dp")
     me = lax.axis_index("seq")
@@ -69,6 +71,18 @@
     head_dim = width // HEADS
     scale = head_dim ** (-0.5)
 
+    square = seq == 4 and base == 2
+    direct = (1, 2) if square else tuple(range(1, seq))
+    half = patches // 2
+    loads = [
+        pltpu.make_async_copy(away, near, load_sem.at[i])
+        for i, (away, near) in enumerate(
+            zip((h_si, h_ni, h_so, h_no, h_mi, h_mo), (sig_in, noi_in, sig_out, noi_out, mean_in, mean_out))
+        )
+    ]
+    for load in loads:
+        load.start()
+
     def shifted(k, sign):
         row = (me // base + sign * (k // base) + tall) % tall
         return row * base + (me % base + sign * (k % base) + base) % base
@@ -109,7 +123,18 @@
             nrm_all.at[me], nrm_all.at[me], nrm_s.at[k], nrm_r.at[me], peer(shifted(k, 1))
         )
 
-    for k in range(1, seq):
+    def relay(buf, k, s, r):
+        part = buf.at[shifted(k, -1), pl.ds((k - 1) * half, half)]
+        return remote(part, part, s.at[k - 1], r.at[k - 1], peer(shifted(3 - k, 1)))
+
+    def relayed(buf, j, r):
+        for i in range(2):
+            arrived(buf.at[j, pl.ds(i * half, half)], r.at[i])
+
+    def arrived(dst, sem):
+        remote(dst, dst, sem, sem, peer(me)).wait_recv()
+
+    for k in direct:
         cot_copy(k).start()
 
     group = LANES // head_dim
@@ -136,12 +161,19 @@
     gain_f = gain[...].astype(F32)
     ahat, _ = norm_stats(resid[...].astype(F32))
     nrm_all[me] = (ahat * gain_f).astype(BF)
-    for k in range(1, seq):
+    for k in direct:
         nrm_copy(k).start()
+    for load in loads:
+        load.wait()
 
     pert_in[...] = (sig_in[...].astype(F32) * noi_in[...].astype(F32)).astype(BF)
     pert_out[...] = (sig_out[...].astype(F32) * noi_out[...].astype(F32)).astype(BF)
     cot_all[me] = cot[0]
+    if square:
+        for k in direct:
+            j = shifted(k, -1)
+            arrived(cot_all.at[j], cot_r.at[j])
+            relay(cot_all, k, cf_s, cf_r).start()
 
     def mix_copy(k, j):
         slot = (k - 1) % slots
@@ -151,16 +183,22 @@
         slot = (k - 1) % slots
         return remote(part_d.at[slot], got_d.at[me], dnr_s.at[slot], dnr_r.at[me], peer(j))
 
-    def arrived(dst, sem):
-        remote(dst, dst, sem, sem, peer(me)).wait_recv()
-
     def signs(ref, j):
         return ref[pl.ds(j, 1), :].astype(F32)
 
     def block(k, first):
         j = me if first else shifted(k, -1)
         s_in, s_mid, s_hid, s_out = signs(f_in, j), signs(f_mid, j), signs(f_hid, j), signs(f_out, j)
-        if not first:
+        if square and not first:
+            @pl.when(k < 3)
+            def _():
+                arrived(nrm_all.at[j], nrm_r.at[j])
+                relay(nrm_all, k, nf_s, nf_r).start()
+
+            @pl.when(k == 3)
+            def _():
+                relayed(nrm_all, j, nf_r)
+        elif not first:
             arrived(nrm_all.at[j], nrm_r.at[j])
         x = nrm_all[j]
         pre = dot(x, mean_in[...]) + dot(x * s_in.astype(BF), pert_in[...]) * s_mid
@@ -181,7 +219,12 @@
 
             part_m[(k - 1) % slots] = mixed
             mix_copy(k, j).start()
-            arrived(cot_all.at[j], cot_r.at[j])
+            if square:
+                @pl.when(k == 3)
+                def _():
+                    relayed(cot_all, j, cf_r)
+            else:
+                arrived(cot_all.at[j], cot_r.at[j])
         c = cot_all[j]
         dh = dot_last(c, mean_out[...]) + dot_last(c * s_out.astype(BF), pert_out[...]) * s_hid
         d = (dh * slope).astype(BF)
@@ -314,8 +357,11 @@
     produce(0, hid, cot_all)
     produce(2, nrm_all, dpre)
     merge(0)
-    for k in range(1, seq):
+    for k in direct:
         nrm_copy(k).wait_send()
+        if square:
+            relay(nrm_all, k, nf_s, nf_r).wait_send()
+            relay(cot_all, k, cf_s, cf_r).wait_send()
     cot_all[...] = cot_all[...] * f_out[...].astype(F32).astype(BF)[:, None, :]
     produce(1, hid_f, cot_all)
     chain(0)
@@ -365,7 +411,7 @@
     for a in range(4):
         drain(a)
 
-    for k in range(1, seq):
+    for k in direct:
         cot_copy(k).wait_send()
     for k in range(max(1, seq - slots), seq):
         mix_copy(k, me).wait_send()
@@ -412,6 +458,7 @@
     dma = pltpu.SemaphoreType.DMA
     full = [(CORES, nz) + c for c in cut]
     scratch = [
+        *[vm(a.shape, BF) for a in args[5:11]],
         vm(mean_in.shape, BF),
         vm(mean_out.shape, BF),
         vm((patches, width), BF),
@@ -431,6 +478,8 @@
         dma((4,)), dma((4,)),
         *[dma((4, nz)) for _ in range(10)],
         dma((4,)),
+        *[dma((2,)) for _ in range(4)],
+        dma((6,)),
     ]
     whole = pl.BlockSpec(memory_space=pltpu.VMEM)
     away = pl.BlockSpec(memory_space=pl.ANY)
@@ -438,7 +487,7 @@
         functools.partial(kernel, dp, seq),
         out_shape=[jax.ShapeDtypeStruct(tokens.shape, BF)] * 2
         + [jax.ShapeDtypeStruct(f, BF) for f in full],
-        in_specs=[whole] * 16,
+        in_specs=[whole] * 5 + [away] * 6 + [whole] * 5,
         out_specs=[whole, whole] + [away] * 4,
         scratch_shapes=scratch,
         compiler_params=pltpu.CompilerParams(

time: 164 us -> 172 us (1.049)
  Pallas kernels: 152 us -> 159 us
    pallas_call x1, Pallas kernels: 152 us -> 159 us  [body(): pl.pallas_call(functools.partial(kernel, dp, seq), out_shape=[jax.ShapeDt...]
where the time goes in v2:
time: 172 us
  Pallas kernels  159 us (92%)
  other arithmetic  8.09 us (5%)
  local copies, waits for them, and re-layouts  3.53 us (2%)
    pallas_call x1, Pallas kernels, body(): pl.pallas_call(functools.partial(kernel, dp, seq), out_shape=[jax.ShapeDt...  159 us
    convert_element_type x2, other arithmetic, assemble(): return g.reshape(r, c).astype(F32)  4.61 us

profile of v2, /device:TPU:0, one launch (start us, length us, event | category | flops | bytes accessed | tf_op | source)
XLA Modules:
  0.0 171.6 jit_solution(15700698957872784207)
XLA Ops:
  0.6 1.3 reshape.27.gain
  1.9 159.3 %shard_map.199 = (bf16[1,256,1024]{2,1,0:T(8,128)(2,1)}, bf16[1,256,1024]{2,1,0:T(8,128)(2,1)}, bf16[2,4,64,1024]{3,2,1,0:T(8,128)(2,1)}, bf16[2,4,64,1024]{3,2,...) custom-call(bf16[1,256,1024]{2,1,0:T(8,128)(2,1)} %tok.1, ...), custom_call_target="tpu_custom_call" | custom-call | tf_op jit(solution)/shard_map/pallas_call | solution.py:486
  161.2 0.0 copy-start
  161.2 0.0 copy-start.4
  161.2 3.0 %bitcast_convert_fusion.1 = f32[1024,512]{1,0:T(8,128)} fusion(bf16[2,4,128,512]{3,2,1,0:T(8,128)(2,1)} %get-tuple-element.14), kind=kLoop, calls=%fused_computation.3 | loop fusion | flops 524288 | bytes 3145728 | tf_op jit(solution)/shard_map/convert_element_type | solution.py:503
  164.2 0.0 copy-done
  164.2 0.0 copy-done.4
  164.2 0.0 copy-start.2
  164.2 1.7 convert_multiply_fusion.1
  165.9 0.0 copy-done.2
  165.9 0.0 copy-start.1
  165.9 0.0 copy-start.3
  165.9 1.6 bitcast_convert_fusion
  167.6 0.0 copy-done.1
  167.6 0.6 copy-done.3
  168.2 0.0 copy-start.6
  168.2 0.0 copy-start.5
  168.2 1.8 %convert_multiply_fusion = f32[512,1024]{1,0:T(8,128)} fusion(bf16[512,1024]{1,0:T(8,128)(2,1)S(1)} %copy-done.1, bf16[2,4,64,1024]{3,2,1,0:T(8,128)(2,1)S(1)} %copy-done.3), kind=kLoop, calls=%fused_computation | loop fusion | flops 1572864 | bytes 4194304 | tf_op jit(solution)/shard_map/mul | solution.py:511
  170.0 0.0 copy-done.6
  170.0 0.8 copy.24
  170.8 0.0 copy-done.5
  170.8 0.8 copy.25
Async XLA Ops:
  161.2 3.0 %copy-start = (bf16[1024,512]{1,0:T(8,128)(2,1)S(1)}, bf16[1024,512]{1,0:T(8,128)(2,1)}, u32[]{:S(2)}) copy-start(bf16[1024,512]{1,0:T(8,128)(2,1)} %h_ni.1) | copy-start | bytes 3145732
  161.2 3.0 %copy-start.4 = (bf16[2,4,128,512]{3,2,1,0:T(8,128)(2,1)S(1)}, bf16[2,4,128,512]{3,2,1,0:T(8,128)(2,1)}, u32[]{:S(2)}) copy-start(bf16[2,4,128,512]{3,2,1,0:T(8,128)(2,1)} %get-tuple-element.15) | copy-start | bytes 3145732
  164.2 1.7 %copy-start.2 = (bf16[2,4,64,1024]{3,2,1,0:T(8,128)(2,1)S(1)}, bf16[2,4,64,1024]{3,2,1,0:T(8,128)(2,1)}, u32[]{:S(2)}) copy-start(bf16[2,4,64,1024]{3,2,1,0:T(8,128)(2,1)} %get-tuple-element.16) | copy-start | bytes 3145732
  165.9 1.6 copy-start.1
  165.9 2.3 %copy-start.3 = (bf16[2,4,64,1024]{3,2,1,0:T(8,128)(2,1)S(1)}, bf16[2,4,64,1024]{3,2,1,0:T(8,128)(2,1)}, u32[]{:S(2)}) copy-start(bf16[2,4,64,1024]{3,2,1,0:T(8,128)(2,1)} %get-tuple-element.17) | copy-start | bytes 3145732
  168.2 1.8 %copy-start.6 = (bf16[1,256,1024]{2,1,0:T(8,128)(2,1)S(1)}, bf16[1,256,1024]{2,1,0:T(8,128)(2,1)}, u32[]{:S(2)}) copy-start(bf16[1,256,1024]{2,1,0:T(8,128)(2,1)} %get-tuple-element.24) | copy-start | bytes 1572868
  168.2 2.6 %copy-start.5 = (bf16[1,256,1024]{2,1,0:T(8,128)(2,1)S(1)}, bf16[1,256,1024]{2,1,0:T(8,128)(2,1)}, u32[]{:S(2)}) copy-start(bf16[1,256,1024]{2,1,0:T(8,128)(2,1)} %get-tuple-element.25) | copy-start | bytes 1572868
